TPU v7x, 512 devices: a whole 4x4x16 slice. The times are simulated.
512 devices in a mesh: ell: 16 (over y, z_lo), blk: 32 (over x, z_hi, core).
Axes of the slice: x: 4, y: 4, z: 16 (z_hi: 4, z_lo: 4; z = z_hi * 4 + z_lo), core: 2. Of those that a mesh axis runs over, the one named last changes fastest.
Arguments:
- wigner: bfloat16 [32, 17, 2162688], P(None, None, ('ell', 'blk')), may hold values from -6 to 6
- sky_alm: float32 [2, 2162688], P(None, ('ell', 'blk')), may hold values from -0.03125 to 0.03125
- beam_blm: float32 [2, 17, 2048], replicated, may hold values from -4.25 to 4.25
- slot_col: int32 [2162688], P(('ell', 'blk')), may hold values from -1 to 63, as said below
- slot_ell: int32 [2162688], P(('ell', 'blk')), may hold values from 0 to 2047, as said below
- order_of_column: int32 [2048], replicated, may hold values from 0 to 2047, as said below
Outputs:
- conv_cube: float32 [32, 32, 4096], P('ell', 'blk')
Inputs may be any that keep to these rules, and one draw needn't show every extreme that they name: `slot_col`: slot block b (slots b * 4224 to b * 4224 + 4223) belongs to ell index b // 32 and blk index b % 32; at most 4098 slots of a block are live, and some blocks have exactly that many. `slot_ell`: every pair (l, m) with m <= l < 2048 stands in exactly one live slot; within a blk group, higher ell indices hold degrees no lower than those of lower ell indices. `order_of_column`: A permutation of 0 to 2047; every blk group's orders hold the same number of pairs.
All inputs are finite; a program needn't handle non-finite values.
Results may differ from a plain program's by a relative error of at most 0.0029.
Values sent between devices are 32-bit elements; how exact they have to be, the bound alone decides.
A program may use at most 64 MiB of HBM per device.

v0:
```python
import math

import jax
import jax.numpy as jnp
import numpy as np
from jax import lax
from jax.experimental import pallas as pl
from jax.experimental.pallas import tpu as pltpu
from jax.sharding import PartitionSpec as P

F32, BF16, I32 = jnp.float32, jnp.bfloat16, jnp.int32
MESH = pl.DeviceIdType.MESH
K, T, C = 17, 32, 64
BLKS = 32

def build_table(beam, table):
    rows = jnp.concatenate([beam[:, 0, :], beam[:, 1, :], jnp.zeros((6, 2048), F32)], axis=0)
    high = rows.astype(BF16)
    low = (rows - high.astype(F32)).astype(BF16)
    for h in range(16):
        span = slice(h * 128, h * 128 + 128)
        table[h, :, 0:128] = high[:, span]
        table[h, :, 128:256] = low[:, span]


def gather_block(base, table, ell, sky, coef, row, cols):
    n = 128 * cols
    degree = jnp.concatenate([ell[pl.ds(row + c, 1), :] for c in range(cols)], axis=1)
    low = degree & 127
    high = (degree >> 7) - base
    hot = (lax.broadcasted_iota(I32, (128, n), 0) == low).astype(F32).astype(BF16)
    hot = jnp.concatenate([hot, hot], axis=0)
    lhs = table[pl.ds(base, 10)].reshape(10 * 40, 256)
    picked = jnp.dot(lhs, hot, preferred_element_type=F32)
    total = jnp.zeros((40, n), F32)
    for h in range(10):
        total = jnp.where(high == h, picked[h * 40 : h * 40 + 40], total)
    br, bi = total[0:17], total[17:34]
    start = pl.multiple_of(row * 128, 128)
    s0 = sky[0:1, pl.ds(start, n)]
    s1 = sky[1:2, pl.ds(start, n)]
    coef[0, 0:17, pl.ds(start, n)] = s0 * br - s1 * bi
    coef[1, 0:17, pl.ds(start, n)] = s0 * bi + s1 * br


def add_block(wig, coef, col, acc, row, cols):
    lhs = []
    rhs = []
    zero = jnp.zeros((64, 128), BF16)
    for c in range(cols):
        start = pl.multiple_of((row + c) * 128, 128)
        span = pl.ds(start, 128)
        re, im = [], []
        for k in range(K):
            w = wig[k, :, span].astype(F32)
            re.append((w * coef[0, pl.ds(k, 1), span]).astype(BF16))
            im.append((w * coef[1, pl.ds(k, 1), span]).astype(BF16))
        lhs += [jnp.concatenate(re, axis=0), jnp.concatenate(im, axis=0)]
        hot = (lax.broadcasted_iota(I32, (64, 128), 0) == col[pl.ds(row + c, 1), :]).astype(F32).astype(BF16)
        rhs += [jnp.concatenate([hot, zero], axis=0), jnp.concatenate([zero, hot], axis=0)]
    left = jnp.concatenate(lhs, axis=1)
    right = jnp.concatenate(rhs, axis=1)
    part = lax.dot_general(left, right, (((1,), (1,)), ((), ())), preferred_element_type=F32)
    acc[...] += part.reshape(K, T, 128)


def gather_all(sky, beam, col, ell, table, coef):
    build_table(beam, table)
    base = jnp.minimum(jnp.min(jnp.where(col[...] >= 0, ell[...], 2047)) >> 7, 6)
    gather_block(base, table, ell, sky, coef, 0, ell.shape[0])


def add_all(wig, col, coef, acc):
    acc[...] = jnp.zeros((K, T, 128), F32)
    add_block(wig, coef, col, acc, 0, col.shape[0])


def constants():
    out = np.zeros((448, 128), np.float64)
    for p in range(32):
        for tt in range(2):
            for k in range(K):
                at = tt * 16 + k if k < 16 else 32 + tt
                angle = 2.0 * math.pi * (k * p % 32) / 32
                out[p * 2 + tt, at] = math.cos(angle)
                out[64 + p * 2 + tt, at] = math.sin(angle)
    n = np.arange(64)
    angle = 2.0 * math.pi * (np.outer(n, np.arange(32)) % 64) / 64
    out[128:192, :32] = np.cos(angle)
    out[192:256, :32] = np.sin(angle)
    angle = 2.0 * math.pi * np.outer(n, n) / 4096
    out[256:320] = np.concatenate([np.cos(angle), np.cos(angle)], 1)
    out[320:384] = np.concatenate([-np.sin(angle), np.sin(angle)], 1)
    w = np.concatenate([n[0::2], n[1::2]])
    angle = 2.0 * math.pi * (np.outer(w, n) % 64) / 64
    out[384:448] = np.concatenate([np.cos(angle), -np.sin(angle)], 1)
    return out.astype(np.float32)


def dot_exact(a, b, contract=((1,), (0,))):
    return lax.dot_general(
        a, b, (contract, ((), ())), precision=lax.Precision.HIGHEST, preferred_element_type=F32
    )


def rotated(x):
    return pltpu.roll(x, 64, 1)


def turned(both, sign):
    half = both.shape[0] // 2
    return both[:half] + sign * rotated(both[half:])


def kernel(
    wig_hbm, sky_hbm, beam_hbm, col_hbm, ell_hbm, ooc_hbm, const_hbm,
    left_ref, right_ref,
    wig, sky, beam, col, ell, ooc, const,
    table, coef, acc, from_y, hy, to_z, from_z, ps, got, key, hot_low, grid,
    in_sem, y_send, y_recv, z_send, z_recv, b_send, b_recv,
):
    e = lax.axis_index("ell")
    b = lax.axis_index("blk")
    y, z = e // 4, e % 4
    x, zh, core = b // 8, (b // 2) % 4, b % 2

    def y_peer(d):
        return (lax.rem(y + d, 4) * 4 + z, b)

    def z_peer(d):
        return (y * 4 + lax.rem(z + d, 4), b)

    def b_peer(d):
        return (e, lax.rem(b + d, BLKS))

    loads = [
        pltpu.make_async_copy(src, dst, in_sem.at[i])
        for i, (src, dst) in enumerate(
            [
                (beam_hbm, beam), (ell_hbm, ell), (col_hbm, col), (sky_hbm, sky),
                (const_hbm, const), (ooc_hbm, ooc), (wig_hbm, wig),
            ]
        )
    ]
    for load in loads:
        load.start()
    barrier = pltpu.get_barrier_semaphore()
    peers = [y_peer(d) for d in range(1, 4)] + [z_peer(d) for d in range(1, 4)]
    peers += [b_peer(d) for d in range(1, BLKS)]
    for peer in peers:
        pl.semaphore_signal(barrier, inc=1, device_id=peer, device_id_type=MESH)
    for load in loads[:-1]:
        load.wait()
    gather_all(sky, beam, col, ell, table, coef)
    loads[-1].wait()
    add_all(wig, col, coef, acc)

    pl.semaphore_wait(barrier, len(peers))

    def y_copy(d):
        there = pl.multiple_of(lax.rem(y + d, 4) * 8, 8)
        return pltpu.make_async_remote_copy(
            src_ref=acc.at[:, pl.ds(there, 8), :], dst_ref=from_y.at[d - 1],
            send_sem=y_send.at[d - 1], recv_sem=y_recv.at[d - 1],
            device_id=y_peer(d), device_id_type=MESH,
        )

    y_copies = [y_copy(d) for d in (2, 1, 3)]
    for copy in y_copies:
        copy.start()

    lane = lax.broadcasted_iota(I32, (16, 128), 1)
    order = ooc[...]
    swapped = rotated(order)
    even = jnp.where(lane < 64, order, swapped)
    odd = jnp.where(lane < 64, swapped, order)
    side = jnp.where(lane < 64, 0, 64)
    key[0] = (even & 63) + side
    key[1] = (odd & 63) + side
    key[2] = even >> 6
    key[3] = odd >> 6
    rows = lax.broadcasted_iota(I32, (128, 128), 0)

    def low_step(a, _):
        hot_low[a, :, 0:128] = (rows == key[0, pl.ds(a, 1), :]).astype(F32).astype(BF16)
        hot_low[a, :, 128:256] = (rows == key[1, pl.ds(a, 1), :]).astype(F32).astype(BF16)
        return 0

    lax.fori_loop(0, 16, low_step, 0)
    grid[...] = jnp.zeros((64, 128), F32)
    to_z[:, 32:40, :] = jnp.zeros((4, 8, 128), F32)

    for copy in y_copies:
        copy.wait_recv()
    mine = pl.multiple_of(y * 8, 8)
    total = acc[:, pl.ds(mine, 8), :] + from_y[0] + from_y[1] + from_y[2]
    hy[...] = total.reshape(K * 8, 128)
    for d in range(4):
        for tt in range(2):
            at = 2 * d + tt
            to_z[d, tt * 16 : tt * 16 + 8, :] = hy[pl.ds(at, 8, stride=8), :]
            to_z[d, tt * 16 + 8 : tt * 16 + 16, :] = hy[pl.ds(64 + at, 8, stride=8), :]
            to_z[d, 32 + tt : 33 + tt, :] = hy[128 + at : 129 + at, :]

    def z_copy(d):
        return pltpu.make_async_remote_copy(
            src_ref=to_z.at[lax.rem(z + d, 4)], dst_ref=from_z.at[d - 1],
            send_sem=z_send.at[d - 1], recv_sem=z_recv.at[d - 1],
            device_id=z_peer(d), device_id_type=MESH,
        )

    z_copies = [z_copy(d) for d in (2, 1, 3)]
    for copy in z_copies:
        copy.start()
    for copy in z_copies:
        copy.wait_recv()
    summed = to_z[z] + from_z[0] + from_z[1] + from_z[2]
    lanes = lax.broadcasted_iota(I32, (1, 128), 1)
    sign = jnp.where(lanes < 64, -1.0, 1.0).astype(F32)
    psi = turned(dot_exact(const[0:128, 0:40], summed), sign)
    for p in range(BLKS):
        ps[p] = psi[2 * p : 2 * p + 2]

    def b_copy(d):
        there = lax.rem(b + d, BLKS)
        return pltpu.make_async_remote_copy(
            src_ref=ps.at[there], dst_ref=got.at[b],
            send_sem=b_send.at[d], recv_sem=b_recv.at[b],
            device_id=b_peer(d), device_id_type=MESH,
        )

    b_copies = [b_copy(d) for d in range(1, BLKS)]
    for copy in b_copies:
        copy.start()
    got[b] = ps[b]

    highs = lax.broadcasted_iota(I32, (32, 128), 0)
    steps = sorted(
        ((dx, dz) for dx in range(4) for dz in range(4)),
        key=lambda s: min(s[0], 4 - s[0]) + 4 * min(s[1], 4 - s[1]),
    )
    for dx, dz in steps:
        chip = lax.rem(x + dx, 4) * 4 + lax.rem(zh + dz, 4)
        for c in range(2):
            source = chip * 2 + c
            arrival = pltpu.make_async_remote_copy(
                src_ref=ps.at[0], dst_ref=got.at[source],
                send_sem=b_send.at[0], recv_sem=b_recv.at[source],
                device_id=(e, source), device_id_type=MESH,
            )
            if (dx, dz) == (0, 0):
                @pl.when(core != c)
                def _():
                    arrival.wait_recv()
            else:
                arrival.wait_recv()
        parts = []
        for c in range(2):
            value = got[chip * 2 + c]
            here = highs == key[2 + c, pl.ds(chip, 1), :]
            spread = jnp.concatenate(
                [jnp.where(here, value[tt : tt + 1, :], 0.0) for tt in range(2)], axis=0
            )
            high = spread.astype(BF16)
            parts.append(jnp.concatenate([high, (spread - high.astype(F32)).astype(BF16)], axis=0))
        placed = lax.dot_general(
            jnp.concatenate(parts, axis=1), hot_low[chip], (((1,), (1,)), ((), ())),
            preferred_element_type=F32,
        )
        grid[...] += placed[0:64] + placed[64:128]

    results = []
    for tt in range(2):
        first = turned(dot_exact(const[128:256, 0:32], grid[tt * 32 : tt * 32 + 32, :]), sign)
        results.append(first * const[256:320, :] + rotated(first) * const[320:384, :])
    last = dot_exact(const[384:448, :], jnp.concatenate(results, axis=0), ((1,), (1,)))
    low, upp = last[0:32], last[32:64]
    left = lax.broadcasted_iota(I32, (32, 128), 1) < 64
    left_ref[0] = jnp.where(left, low, 0.0)
    right_ref[0] = jnp.where(left, 0.0, rotated(upp))
    left_ref[1] = jnp.where(left, rotated(low), 0.0)
    right_ref[1] = jnp.where(left, 0.0, upp)
    for copy in y_copies + z_copies + b_copies:
        copy.wait_send()


def on_device(wigner, sky_alm, beam_blm, slot_col, slot_ell, order_of_column):
    q = wigner.shape[2]
    any_space = pl.BlockSpec(memory_space=pltpu.HBM)
    dma = pltpu.SemaphoreType.DMA
    left, right = pl.pallas_call(
        kernel,
        out_shape=[jax.ShapeDtypeStruct((2, 32, 128), F32)] * 2,
        in_specs=[any_space] * 7,
        out_specs=[pl.BlockSpec(memory_space=pltpu.VMEM)] * 2,
        scratch_shapes=[
            pltpu.VMEM((K, T, q), BF16),
            pltpu.VMEM((2, q), F32),
            pltpu.VMEM((K, 2, 2048), F32),
            pltpu.VMEM((q // 128, 128), I32),
            pltpu.VMEM((q // 128, 128), I32),
            pltpu.VMEM((16, 128), I32),
            pltpu.VMEM((448, 128), F32),
            pltpu.VMEM((16, 40, 256), BF16),
            pltpu.VMEM((2, 24, q), F32),
            pltpu.VMEM((K, T, 128), F32),
            pltpu.VMEM((3, K, 8, 128), F32),
            pltpu.VMEM((K * 8, 128), F32),
            pltpu.VMEM((4, 40, 128), F32),
            pltpu.VMEM((3, 40, 128), F32),
            pltpu.VMEM((BLKS, 2, 128), F32),
            pltpu.VMEM((BLKS, 2, 128), F32),
            pltpu.VMEM((4, 16, 128), I32),
            pltpu.VMEM((16, 128, 256), BF16),
            pltpu.VMEM((64, 128), F32),
            dma((7,)),
            dma((3,)), dma((3,)), dma((3,)), dma((3,)), dma((BLKS,)), dma((BLKS,)),
        ],
        compiler_params=pltpu.CompilerParams(
            collective_id=0, has_side_effects=True, vmem_limit_bytes=40 * 1024 * 1024
        ),
    )(
        *(
            pltpu.with_memory_space_constraint(operand, pltpu.HBM)
            for operand in (
                jnp.transpose(wigner, (1, 0, 2)),
                sky_alm,
                jnp.transpose(beam_blm, (1, 0, 2)),
                slot_col.reshape(q // 128, 128),
                slot_ell.reshape(q // 128, 128),
                order_of_column.reshape(16, 128),
                jnp.asarray(constants()),
            )
        )
    )
    return left.reshape(2, 1, 4096) + right.reshape(2, 1, 4096)


def solution(mesh):
    return jax.shard_map(
        on_device,
        mesh=mesh,
        in_specs=(
            P(None, None, ("ell", "blk")),
            P(None, ("ell", "blk")),
            P(),
            P(("ell", "blk")),
            P(("ell", "blk")),
            P(),
        ),
        out_specs=P("ell", "blk", None),
        check_vma=False,
    )
```

profile of v0, /device:TPU:1, one launch (start us, length us, event | category | flops | bytes accessed | tf_op | source)
XLA Modules:
  0.0 38.4 jit_solution(3404242213917492178)
XLA Ops:
  0.0 37.8 %shard_map.73 = (f32[2,32,128]{2,1,0:T(8,128)S(1)}, f32[2,32,128]{2,1,0:T(8,128)S(1)}) custom-call(bf16[17,32,4224]{2,1,0:T(8,128)(2,1)} %bitcast.6, f32[2,4224]{1,0:T(2,128)} %sky_hbm.1, f32[17,2,2048]{2,1,0:T(2,128)} %bitcast.7, s32[33,128]{1,0:T(8,128)} %bitcast.8, s32[33,128]{1,0:T(8,128)} %bitcast.9, s32[16,128]{1,0:T(8,128)} %bitcast.10, ...), custom_call_target="tpu_custom_call" | custom-call | tf_op jit(solution)/shard_map/pallas_call | solution.py:291
  37.8 0.6 %add.14 = f32[2,32,128]{2,1,0:T(8,128)} add(f32[2,32,128]{2,1,0:T(8,128)S(1)} %get-tuple-element.7, f32[2,32,128]{2,1,0:T(8,128)S(1)} %get-tuple-element.8) | non-fusion elementwise | flops 8192 | bytes 98304 | tf_op jit(solution)/shard_map/add | solution.py:336
where the time goes:
time: 38.5 us; the launch traced here: 38.4 us
  Pallas kernels  37.8 us (98%)
  other arithmetic  0.62 us (2%)
    pallas_call x1, Pallas kernels, on_device(): pl.pallas_call(kernel, out_shape=[jax.ShapeDtypeStruct((2, 32, 128), F32)...  37.8 us

commit v1 on v0

--- a/solution.py
+++ b/solution.py
@@ -11,6 +11,7 @@
 F32, BF16, I32 = jnp.float32, jnp.bfloat16, jnp.int32
 MESH = pl.DeviceIdType.MESH
 K, T, C = 17, 32, 64
+H = 8
 BLKS = 32
 
 def build_table(beam, table):
@@ -80,7 +81,7 @@
     for p in range(32):
         for tt in range(2):
             for k in range(K):
-                at = tt * 16 + k if k < 16 else 32 + tt
+                at = tt * H + k if k < H else 2 * k + tt
                 angle = 2.0 * math.pi * (k * p % 32) / 32
                 out[p * 2 + tt, at] = math.cos(angle)
                 out[64 + p * 2 + tt, at] = math.sin(angle)
@@ -116,22 +117,29 @@
     wig_hbm, sky_hbm, beam_hbm, col_hbm, ell_hbm, ooc_hbm, const_hbm,
     left_ref, right_ref,
     wig, sky, beam, col, ell, ooc, const,
-    table, coef, acc, from_y, hy, to_z, from_z, ps, got, key, hot_low, grid,
-    in_sem, y_send, y_recv, z_send, z_recv, b_send, b_recv,
+    table, coef, acc, to_ell, from_ell, from_y, by_cycle, to_z, from_z, summed, ps, got, key, hot_low, grid,
+    in_sem, e_send, e_recv, y_send, y_recv, z_send, z_recv, b_send, b_recv,
 ):
     e = lax.axis_index("ell")
     b = lax.axis_index("blk")
     y, z = e // 4, e % 4
     x, zh, core = b // 8, (b // 2) % 4, b % 2
 
-    def y_peer(d):
-        return (lax.rem(y + d, 4) * 4 + z, b)
-
-    def z_peer(d):
-        return (y * 4 + lax.rem(z + d, 4), b)
-
-    def b_peer(d):
-        return (e, lax.rem(b + d, BLKS))
+    def others(order, place):
+        return [
+            jnp.where(place <= i, order[i + 1], order[i]).astype(I32) for i in range(len(order) - 1)
+        ]
+
+    def swap(i):
+        return i + (i // 2) * (5 - 2 * i)
+
+    owners = others([there * 4 + at for at in range(4) for there in range(4)], z * 4 + y)
+    chips = [xs * 4 + zs for zs in (0, 1, 3, 2) for xs in (0, 1, 3, 2)]
+    members = others(
+        [chip * 2 + c for chip in chips for c in (1, 0)], swap(zh) * 8 + swap(x) * 2 + 1 - core
+    )
+    rows_y = others(list(range(4)), y)
+    runs_z = others(list(range(4)), z)
 
     loads = [
         pltpu.make_async_copy(src, dst, in_sem.at[i])
@@ -145,9 +153,9 @@
     for load in loads:
         load.start()
     barrier = pltpu.get_barrier_semaphore()
-    peers = [y_peer(d) for d in range(1, 4)] + [z_peer(d) for d in range(1, 4)]
-    peers += [b_peer(d) for d in range(1, BLKS)]
-    for peer in peers:
+    peers = [(owner, b) for owner in owners]
+    peers += [(e, there) for there in members]
+    for peer in reversed(peers):
         pl.semaphore_signal(barrier, inc=1, device_id=peer, device_id_type=MESH)
     for load in loads[:-1]:
         load.wait()
@@ -157,16 +165,30 @@
 
     pl.semaphore_wait(barrier, len(peers))
 
-    def y_copy(d):
-        there = pl.multiple_of(lax.rem(y + d, 4) * 8, 8)
+    def y_copy(i):
+        there = rows_y[i]
         return pltpu.make_async_remote_copy(
-            src_ref=acc.at[:, pl.ds(there, 8), :], dst_ref=from_y.at[d - 1],
-            send_sem=y_send.at[d - 1], recv_sem=y_recv.at[d - 1],
-            device_id=y_peer(d), device_id_type=MESH,
-        )
-
-    y_copies = [y_copy(d) for d in (2, 1, 3)]
+            src_ref=acc.at[0:H, pl.ds(pl.multiple_of(there * 8, 8), 8), :], dst_ref=from_y.at[y],
+            send_sem=y_send.at[i], recv_sem=y_recv.at[y],
+            device_id=(there * 4 + z, b), device_id_type=MESH,
+        )
+
+    y_copies = [y_copy(i) for i in range(3)]
     for copy in y_copies:
+        copy.start()
+    for k in range(H, K):
+        for owner in range(16):
+            to_ell[owner, k - H] = acc[k, 2 * owner : 2 * owner + 2, :]
+
+    def e_copy(i):
+        return pltpu.make_async_remote_copy(
+            src_ref=to_ell.at[owners[i]], dst_ref=from_ell.at[e],
+            send_sem=e_send.at[i], recv_sem=e_recv.at[e],
+            device_id=(owners[i], b), device_id_type=MESH,
+        )
+
+    e_copies = [e_copy(i) for i in range(15)]
+    for copy in e_copies:
         copy.start()
 
     lane = lax.broadcasted_iota(I32, (16, 128), 1)
@@ -188,76 +210,88 @@
 
     lax.fori_loop(0, 16, low_step, 0)
     grid[...] = jnp.zeros((64, 128), F32)
-    to_z[:, 32:40, :] = jnp.zeros((4, 8, 128), F32)
-
-    for copy in y_copies:
-        copy.wait_recv()
-    mine = pl.multiple_of(y * 8, 8)
-    total = acc[:, pl.ds(mine, 8), :] + from_y[0] + from_y[1] + from_y[2]
-    hy[...] = total.reshape(K * 8, 128)
+    summed[32:40, :] = jnp.zeros((8, 128), F32)
+
+    mine = acc[0:H, pl.ds(pl.multiple_of(y * 8, 8), 8), :]
+    for there in rows_y:
+        pltpu.make_async_remote_copy(
+            src_ref=from_y.at[0], dst_ref=from_y.at[there],
+            send_sem=y_send.at[0], recv_sem=y_recv.at[there],
+            device_id=(there * 4 + z, b), device_id_type=MESH,
+        ).wait_recv()
+        mine = mine + from_y[there]
+    by_cycle[...] = mine.reshape(H * 8, 128)
     for d in range(4):
         for tt in range(2):
-            at = 2 * d + tt
-            to_z[d, tt * 16 : tt * 16 + 8, :] = hy[pl.ds(at, 8, stride=8), :]
-            to_z[d, tt * 16 + 8 : tt * 16 + 16, :] = hy[pl.ds(64 + at, 8, stride=8), :]
-            to_z[d, 32 + tt : 33 + tt, :] = hy[128 + at : 129 + at, :]
-
-    def z_copy(d):
+            to_z[d, tt * 8 : tt * 8 + 8, :] = by_cycle[pl.ds(2 * d + tt, 8, stride=8), :]
+
+    def z_copy(i):
+        there = runs_z[i]
         return pltpu.make_async_remote_copy(
-            src_ref=to_z.at[lax.rem(z + d, 4)], dst_ref=from_z.at[d - 1],
-            send_sem=z_send.at[d - 1], recv_sem=z_recv.at[d - 1],
-            device_id=z_peer(d), device_id_type=MESH,
-        )
-
-    z_copies = [z_copy(d) for d in (2, 1, 3)]
+            src_ref=to_z.at[there], dst_ref=from_z.at[z],
+            send_sem=z_send.at[i], recv_sem=z_recv.at[z],
+            device_id=(y * 4 + there, b), device_id_type=MESH,
+        )
+
+    z_copies = [z_copy(i) for i in range(3)]
     for copy in z_copies:
         copy.start()
-    for copy in z_copies:
-        copy.wait_recv()
-    summed = to_z[z] + from_z[0] + from_z[1] + from_z[2]
+    total = to_ell[e]
+    for owner in reversed(owners):
+        pltpu.make_async_remote_copy(
+            src_ref=to_ell.at[0], dst_ref=from_ell.at[owner],
+            send_sem=e_send.at[0], recv_sem=e_recv.at[owner],
+            device_id=(owner, b), device_id_type=MESH,
+        ).wait_recv()
+        total = total + from_ell[owner]
+    for k in range(H, K):
+        summed[2 * k : 2 * k + 2, :] = total[k - H]
+    joined = to_z[z]
+    for there in runs_z:
+        pltpu.make_async_remote_copy(
+            src_ref=to_z.at[0], dst_ref=from_z.at[there],
+            send_sem=z_send.at[0], recv_sem=z_recv.at[there],
+            device_id=(y * 4 + there, b), device_id_type=MESH,
+        ).wait_recv()
+        joined = joined + from_z[there]
+    summed[0 : 2 * H, :] = joined
     lanes = lax.broadcasted_iota(I32, (1, 128), 1)
     sign = jnp.where(lanes < 64, -1.0, 1.0).astype(F32)
-    psi = turned(dot_exact(const[0:128, 0:40], summed), sign)
+    psi = turned(dot_exact(const[0:128, 0:40], summed[...]), sign)
     for p in range(BLKS):
         ps[p] = psi[2 * p : 2 * p + 2]
 
-    def b_copy(d):
-        there = lax.rem(b + d, BLKS)
+    def b_copy(i):
+        there = members[i]
         return pltpu.make_async_remote_copy(
             src_ref=ps.at[there], dst_ref=got.at[b],
-            send_sem=b_send.at[d], recv_sem=b_recv.at[b],
-            device_id=b_peer(d), device_id_type=MESH,
-        )
-
-    b_copies = [b_copy(d) for d in range(1, BLKS)]
+            send_sem=b_send.at[i], recv_sem=b_recv.at[b],
+            device_id=(e, there), device_id_type=MESH,
+        )
+
+    b_copies = [b_copy(i) for i in range(BLKS - 1)]
     for copy in b_copies:
         copy.start()
     got[b] = ps[b]
 
     highs = lax.broadcasted_iota(I32, (32, 128), 0)
-    steps = sorted(
-        ((dx, dz) for dx in range(4) for dz in range(4)),
-        key=lambda s: min(s[0], 4 - s[0]) + 4 * min(s[1], 4 - s[1]),
-    )
-    for dx, dz in steps:
-        chip = lax.rem(x + dx, 4) * 4 + lax.rem(zh + dz, 4)
+    for chip in chips:
         for c in range(2):
             source = chip * 2 + c
             arrival = pltpu.make_async_remote_copy(
                 src_ref=ps.at[0], dst_ref=got.at[source],
                 send_sem=b_send.at[0], recv_sem=b_recv.at[source],
-                device_id=(e, source), device_id_type=MESH,
+                device_id=(e, members[0]), device_id_type=MESH,
             )
-            if (dx, dz) == (0, 0):
-                @pl.when(core != c)
-                def _():
-                    arrival.wait_recv()
-            else:
+
+            @pl.when(b != source)
+            def _():
                 arrival.wait_recv()
+
         parts = []
         for c in range(2):
             value = got[chip * 2 + c]
-            here = highs == key[2 + c, pl.ds(chip, 1), :]
+            here = highs == key[2 + c, chip : chip + 1, :]
             spread = jnp.concatenate(
                 [jnp.where(here, value[tt : tt + 1, :], 0.0) for tt in range(2)], axis=0
             )
@@ -280,7 +314,7 @@
     right_ref[0] = jnp.where(left, 0.0, rotated(upp))
     left_ref[1] = jnp.where(left, rotated(low), 0.0)
     right_ref[1] = jnp.where(left, 0.0, upp)
-    for copy in y_copies + z_copies + b_copies:
+    for copy in y_copies + z_copies + e_copies + b_copies:
         copy.wait_send()
 
 
@@ -304,17 +338,20 @@
             pltpu.VMEM((16, 40, 256), BF16),
             pltpu.VMEM((2, 24, q), F32),
             pltpu.VMEM((K, T, 128), F32),
-            pltpu.VMEM((3, K, 8, 128), F32),
-            pltpu.VMEM((K * 8, 128), F32),
-            pltpu.VMEM((4, 40, 128), F32),
-            pltpu.VMEM((3, 40, 128), F32),
+            pltpu.VMEM((16, K - H, 2, 128), F32),
+            pltpu.VMEM((16, K - H, 2, 128), F32),
+            pltpu.VMEM((4, H, 8, 128), F32),
+            pltpu.VMEM((H * 8, 128), F32),
+            pltpu.VMEM((4, 2 * H, 128), F32),
+            pltpu.VMEM((4, 2 * H, 128), F32),
+            pltpu.VMEM((40, 128), F32),
             pltpu.VMEM((BLKS, 2, 128), F32),
             pltpu.VMEM((BLKS, 2, 128), F32),
             pltpu.VMEM((4, 16, 128), I32),
             pltpu.VMEM((16, 128, 256), BF16),
             pltpu.VMEM((64, 128), F32),
             dma((7,)),
-            dma((3,)), dma((3,)), dma((3,)), dma((3,)), dma((BLKS,)), dma((BLKS,)),
+            dma((15,)), dma((16,)), dma((3,)), dma((4,)), dma((3,)), dma((4,)), dma((BLKS,)), dma((BLKS,)),
         ],
         compiler_params=pltpu.CompilerParams(
             collective_id=0, has_side_effects=True, vmem_limit_bytes=40 * 1024 * 1024

time: 38.5 us -> 37.4 us (0.971)
  Pallas kernels: 37.8 us -> 36.7 us
    pallas_call x1, Pallas kernels: 37.8 us -> 36.7 us  [on_device(): pl.pallas_call(kernel, out_shape=[jax.ShapeDtypeStruct((2, 32, 128), F32)...]
where the time goes in v1:
time: 37.4 us; the launch traced here: 37.3 us
  Pallas kernels  36.7 us (98%)
  other arithmetic  0.62 us (2%)
    pallas_call x1, Pallas kernels, on_device(): pl.pallas_call(kernel, out_shape=[jax.ShapeDtypeStruct((2, 32, 128), F32)...  36.7 us

profile of v1, /device:TPU:1, one launch (start us, length us, event | category | flops | bytes accessed | tf_op | source)
XLA Modules:
  0.0 37.3 jit_solution(13900039119065455749)
XLA Ops:
  0.0 36.7 %shard_map.73 = (f32[2,32,128]{2,1,0:T(8,128)S(1)}, f32[2,32,128]{2,1,0:T(8,128)S(1)}) custom-call(bf16[17,32,4224]{2,1,0:T(8,128)(2,1)} %bitcast.6, f32[2,4224]{1,0:T(2,128)} %sky_hbm.1, f32[17,2,2048]{2,1,0:T(2,128)} %bitcast.7, s32[33,128]{1,0:T(8,128)} %bitcast.8, s32[33,128]{1,0:T(8,128)} %bitcast.9, s32[16,128]{1,0:T(8,128)} %bitcast.10, ...), custom_call_target="tpu_custom_call" | custom-call | tf_op jit(solution)/shard_map/pallas_call | solution.py:325
  36.7 0.6 %add.14 = f32[2,32,128]{2,1,0:T(8,128)} add(f32[2,32,128]{2,1,0:T(8,128)S(1)} %get-tuple-element.7, f32[2,32,128]{2,1,0:T(8,128)S(1)} %get-tuple-element.8) | non-fusion elementwise | flops 8192 | bytes 98304 | tf_op jit(solution)/shard_map/add | solution.py:373

commit v2 on v1

--- a/solution.py
+++ b/solution.py
@@ -125,6 +125,9 @@
     y, z = e // 4, e % 4
     x, zh, core = b // 8, (b // 2) % 4, b % 2
 
+    turned_run = zh == 2
+    other = y * 4 + 3 - z
+
     def others(order, place):
         return [
             jnp.where(place <= i, order[i + 1], order[i]).astype(I32) for i in range(len(order) - 1)
@@ -133,13 +136,27 @@
     def swap(i):
         return i + (i // 2) * (5 - 2 * i)
 
-    owners = others([there * 4 + at for at in range(4) for there in range(4)], z * 4 + y)
+    def both(order, turned_order, place):
+        return [
+            jnp.where(turned_run, there, here).astype(I32)
+            for here, there in zip(others(order, place), others(turned_order, place))
+        ]
+
+    place_z = jnp.where(turned_run, 3 - z, z).astype(I32)
+    cycles = y * 4 + place_z
+    owned = others([there * 4 + at for at in range(4) for there in range(4)], place_z * 4 + y)
+    owners = both(
+        [there * 4 + at for at in range(4) for there in range(4)],
+        [there * 4 + 3 - at for at in range(4) for there in range(4)],
+        place_z * 4 + y,
+    )
     chips = [xs * 4 + zs for zs in (0, 1, 3, 2) for xs in (0, 1, 3, 2)]
-    members = others(
-        [chip * 2 + c for chip in chips for c in (1, 0)], swap(zh) * 8 + swap(x) * 2 + 1 - core
-    )
+    place_b = swap(zh) * 8 + swap(x) * 2 + 1 - core
+    members = others([chip * 2 + c for chip in chips for c in (1, 0)], place_b)
+    member_turned = others([int(chip % 4 == 2) for chip in chips for c in (1, 0)], place_b)
     rows_y = others(list(range(4)), y)
-    runs_z = others(list(range(4)), z)
+    cycles_z = others(list(range(4)), place_z)
+    runs_z = both(list(range(4)), [3 - at for at in range(4)], place_z)
 
     loads = [
         pltpu.make_async_copy(src, dst, in_sem.at[i])
@@ -154,16 +171,23 @@
         load.start()
     barrier = pltpu.get_barrier_semaphore()
     peers = [(owner, b) for owner in owners]
-    peers += [(e, there) for there in members]
+    peers += [
+        (jnp.where(flag == 1, other, e).astype(I32), there)
+        for there, flag in zip(members, member_turned)
+    ]
     for peer in reversed(peers):
         pl.semaphore_signal(barrier, inc=1, device_id=peer, device_id_type=MESH)
+
+    @pl.when(turned_run)
+    def _():
+        pl.semaphore_signal(barrier, inc=1, device_id=(other, b), device_id_type=MESH)
     for load in loads[:-1]:
         load.wait()
     gather_all(sky, beam, col, ell, table, coef)
     loads[-1].wait()
     add_all(wig, col, coef, acc)
 
-    pl.semaphore_wait(barrier, len(peers))
+    pl.semaphore_wait(barrier, len(peers) + jnp.where(turned_run, 1, 0).astype(I32))
 
     def y_copy(i):
         there = rows_y[i]
@@ -182,8 +206,8 @@
 
     def e_copy(i):
         return pltpu.make_async_remote_copy(
-            src_ref=to_ell.at[owners[i]], dst_ref=from_ell.at[e],
-            send_sem=e_send.at[i], recv_sem=e_recv.at[e],
+            src_ref=to_ell.at[owned[i]], dst_ref=from_ell.at[e],
+            send_sem=e_send.at[0], recv_sem=e_recv.at[e],
             device_id=(owners[i], b), device_id_type=MESH,
         )
 
@@ -228,7 +252,7 @@
     def z_copy(i):
         there = runs_z[i]
         return pltpu.make_async_remote_copy(
-            src_ref=to_z.at[there], dst_ref=from_z.at[z],
+            src_ref=to_z.at[cycles_z[i]], dst_ref=from_z.at[z],
             send_sem=z_send.at[i], recv_sem=z_recv.at[z],
             device_id=(y * 4 + there, b), device_id_type=MESH,
         )
@@ -236,7 +260,7 @@
     z_copies = [z_copy(i) for i in range(3)]
     for copy in z_copies:
         copy.start()
-    total = to_ell[e]
+    total = to_ell[cycles]
     for owner in reversed(owners):
         pltpu.make_async_remote_copy(
             src_ref=to_ell.at[0], dst_ref=from_ell.at[owner],
@@ -246,7 +270,7 @@
         total = total + from_ell[owner]
     for k in range(H, K):
         summed[2 * k : 2 * k + 2, :] = total[k - H]
-    joined = to_z[z]
+    joined = to_z[place_z]
     for there in runs_z:
         pltpu.make_async_remote_copy(
             src_ref=to_z.at[0], dst_ref=from_z.at[there],
@@ -265,14 +289,27 @@
         there = members[i]
         return pltpu.make_async_remote_copy(
             src_ref=ps.at[there], dst_ref=got.at[b],
-            send_sem=b_send.at[i], recv_sem=b_recv.at[b],
-            device_id=(e, there), device_id_type=MESH,
+            send_sem=b_send.at[0], recv_sem=b_recv.at[b],
+            device_id=(cycles, there), device_id_type=MESH,
         )
 
     b_copies = [b_copy(i) for i in range(BLKS - 1)]
     for copy in b_copies:
         copy.start()
-    got[b] = ps[b]
+    home = pltpu.make_async_remote_copy(
+        src_ref=ps.at[b], dst_ref=got.at[b],
+        send_sem=b_send.at[1], recv_sem=b_recv.at[b],
+        device_id=(other, b), device_id_type=MESH,
+    )
+
+    @pl.when(turned_run)
+    def _():
+        home.start()
+
+    @pl.when(zh != 2)
+    def _():
+        got[b] = ps[b]
+
 
     highs = lax.broadcasted_iota(I32, (32, 128), 0)
     for chip in chips:
@@ -284,7 +321,7 @@
                 device_id=(e, members[0]), device_id_type=MESH,
             )
 
-            @pl.when(b != source)
+            @pl.when((b != source) | turned_run)
             def _():
                 arrival.wait_recv()
 
@@ -314,8 +351,20 @@
     right_ref[0] = jnp.where(left, 0.0, rotated(upp))
     left_ref[1] = jnp.where(left, rotated(low), 0.0)
     right_ref[1] = jnp.where(left, 0.0, upp)
-    for copy in y_copies + z_copies + e_copies + b_copies:
+    for copy in y_copies + z_copies:
         copy.wait_send()
+    pltpu.make_async_remote_copy(
+        src_ref=to_ell.at[0:15], dst_ref=from_ell.at[0:15], send_sem=e_send.at[0],
+        recv_sem=e_recv.at[0], device_id=(owners[0], b), device_id_type=MESH,
+    ).wait_send()
+    pltpu.make_async_remote_copy(
+        src_ref=ps.at[0 : BLKS - 1], dst_ref=got.at[0 : BLKS - 1], send_sem=b_send.at[0],
+        recv_sem=b_recv.at[0], device_id=(e, members[0]), device_id_type=MESH,
+    ).wait_send()
+
+    @pl.when(turned_run)
+    def _():
+        home.wait_send()
 
 
 def on_device(wigner, sky_alm, beam_blm, slot_col, slot_ell, order_of_column):
@@ -351,7 +400,7 @@
             pltpu.VMEM((16, 128, 256), BF16),
             pltpu.VMEM((64, 128), F32),
             dma((7,)),
-            dma((15,)), dma((16,)), dma((3,)), dma((4,)), dma((3,)), dma((4,)), dma((BLKS,)), dma((BLKS,)),
+            dma((1,)), dma((16,)), dma((3,)), dma((4,)), dma((3,)), dma((4,)), dma((2,)), dma((BLKS,)),
         ],
         compiler_params=pltpu.CompilerParams(
             collective_id=0, has_side_effects=True, vmem_limit_bytes=40 * 1024 * 1024

time: 37.4 us -> 36 us (0.963)
  Pallas kernels: 36.7 us -> 35.2 us
    pallas_call x1, Pallas kernels: 36.7 us -> 35.2 us  [on_device(): pl.pallas_call(kernel, out_shape=[jax.ShapeDtypeStruct((2, 32, 128), F32)...]
where the time goes in v2:
time: 36 us; the launch traced here: 35.9 us
  Pallas kernels  35.2 us (98%)
  other arithmetic  0.62 us (2%)
    pallas_call x1, Pallas kernels, on_device(): pl.pallas_call(kernel, out_shape=[jax.ShapeDtypeStruct((2, 32, 128), F32)...  35.2 us

profile of v2, /device:TPU:1, one launch (start us, length us, event | category | flops | bytes accessed | tf_op | source)
XLA Modules:
  0.0 35.9 jit_solution(17956525136688573243)
XLA Ops:
  0.0 35.2 %shard_map.73 = (f32[2,32,128]{2,1,0:T(8,128)S(1)}, f32[2,32,128]{2,1,0:T(8,128)S(1)}) custom-call(bf16[17,32,4224]{2,1,0:T(8,128)(2,1)} %bitcast.6, f32[2,4224]{1,0:T(2,128)} %sky_hbm.1, f32[17,2,2048]{2,1,0:T(2,128)} %bitcast.7, s32[33,128]{1,0:T(8,128)} %bitcast.8, s32[33,128]{1,0:T(8,128)} %bitcast.9, s32[16,128]{1,0:T(8,128)} %bitcast.10, ...), custom_call_target="tpu_custom_call" | custom-call | tf_op jit(solution)/shard_map/pallas_call | solution.py:374
  35.2 0.6 %add.14 = f32[2,32,128]{2,1,0:T(8,128)} add(f32[2,32,128]{2,1,0:T(8,128)S(1)} %get-tuple-element.7, f32[2,32,128]{2,1,0:T(8,128)S(1)} %get-tuple-element.8) | non-fusion elementwise | flops 8192 | bytes 98304 | tf_op jit(solution)/shard_map/add | solution.py:422

commit v3 on v2

--- a/solution.py
+++ b/solution.py
@@ -62,7 +62,7 @@
     left = jnp.concatenate(lhs, axis=1)
     right = jnp.concatenate(rhs, axis=1)
     part = lax.dot_general(left, right, (((1,), (1,)), ((), ())), preferred_element_type=F32)
-    acc[...] += part.reshape(K, T, 128)
+    acc[...] = part.reshape(K, T, 128)
 
 
 def gather_all(sky, beam, col, ell, table, coef):
@@ -72,7 +72,6 @@
 
 
 def add_all(wig, col, coef, acc):
-    acc[...] = jnp.zeros((K, T, 128), F32)
     add_block(wig, coef, col, acc, 0, col.shape[0])
 
 
@@ -95,13 +94,25 @@
     w = np.concatenate([n[0::2], n[1::2]])
     angle = 2.0 * math.pi * (np.outer(w, n) % 64) / 64
     out[384:448] = np.concatenate([np.cos(angle), -np.sin(angle)], 1)
-    return out.astype(np.float32)
-
-
-def dot_exact(a, b, contract=((1,), (0,))):
-    return lax.dot_general(
-        a, b, (contract, ((), ())), precision=lax.Precision.HIGHEST, preferred_element_type=F32
-    )
+    twist = jnp.asarray(out[256:384].astype(np.float32))
+    factors = np.zeros((320, 384), jnp.bfloat16)
+    for rows, depth, source in ((128, 48, 0), (128, 32, 128), (64, 128, 384)):
+        at = {0: 0, 128: 128, 384: 256}[source]
+        exact = out[source : source + rows, :depth]
+        high = exact.astype(jnp.bfloat16)
+        low = (exact - high.astype(np.float64)).astype(jnp.bfloat16)
+        factors[at : at + rows, : 3 * depth] = np.concatenate([high, high, low], axis=1)
+    return twist, jnp.asarray(factors)
+
+
+def two_parts(x):
+    high = x.astype(BF16)
+    return [high, (x - high.astype(F32)).astype(BF16)]
+
+
+def three_terms(x, axis):
+    high, low = two_parts(x)
+    return jnp.concatenate([high, low, high], axis=axis)
 
 
 def rotated(x):
@@ -114,9 +125,9 @@
 
 
 def kernel(
-    wig_hbm, sky_hbm, beam_hbm, col_hbm, ell_hbm, ooc_hbm, const_hbm,
+    wig_hbm, sky_hbm, beam_hbm, col_hbm, ell_hbm, ooc_hbm, const_hbm, factors_hbm,
     left_ref, right_ref,
-    wig, sky, beam, col, ell, ooc, const,
+    wig, sky, beam, col, ell, ooc, const, factors,
     table, coef, acc, to_ell, from_ell, from_y, by_cycle, to_z, from_z, summed, ps, got, key, hot_low, grid,
     in_sem, e_send, e_recv, y_send, y_recv, z_send, z_recv, b_send, b_recv,
 ):
@@ -163,7 +174,7 @@
         for i, (src, dst) in enumerate(
             [
                 (beam_hbm, beam), (ell_hbm, ell), (col_hbm, col), (sky_hbm, sky),
-                (const_hbm, const), (ooc_hbm, ooc), (wig_hbm, wig),
+                (const_hbm, const), (ooc_hbm, ooc), (factors_hbm, factors), (wig_hbm, wig),
             ]
         )
     ]
@@ -234,7 +245,7 @@
 
     lax.fori_loop(0, 16, low_step, 0)
     grid[...] = jnp.zeros((64, 128), F32)
-    summed[32:40, :] = jnp.zeros((8, 128), F32)
+    summed[32:48, :] = jnp.zeros((16, 128), F32)
 
     mine = acc[0:H, pl.ds(pl.multiple_of(y * 8, 8), 8), :]
     for there in rows_y:
@@ -281,7 +292,8 @@
     summed[0 : 2 * H, :] = joined
     lanes = lax.broadcasted_iota(I32, (1, 128), 1)
     sign = jnp.where(lanes < 64, -1.0, 1.0).astype(F32)
-    psi = turned(dot_exact(const[0:128, 0:40], summed[...]), sign)
+    terms = three_terms(summed[...], 0)
+    psi = turned(jnp.dot(factors[0:128, 0:144], terms, preferred_element_type=F32), sign)
     for p in range(BLKS):
         ps[p] = psi[2 * p : 2 * p + 2]
 
@@ -312,9 +324,9 @@
 
 
     highs = lax.broadcasted_iota(I32, (32, 128), 0)
-    for chip in chips:
-        for c in range(2):
-            source = chip * 2 + c
+    for first in range(0, 16, 4):
+        group = chips[first : first + 4]
+        for source in [chip * 2 + c for chip in group for c in range(2)]:
             arrival = pltpu.make_async_remote_copy(
                 src_ref=ps.at[0], dst_ref=got.at[source],
                 send_sem=b_send.at[0], recv_sem=b_recv.at[source],
@@ -326,25 +338,30 @@
                 arrival.wait_recv()
 
         parts = []
-        for c in range(2):
-            value = got[chip * 2 + c]
-            here = highs == key[2 + c, chip : chip + 1, :]
-            spread = jnp.concatenate(
-                [jnp.where(here, value[tt : tt + 1, :], 0.0) for tt in range(2)], axis=0
-            )
-            high = spread.astype(BF16)
-            parts.append(jnp.concatenate([high, (spread - high.astype(F32)).astype(BF16)], axis=0))
+        for chip in group:
+            for c in range(2):
+                value = got[chip * 2 + c]
+                here = highs == key[2 + c, chip : chip + 1, :]
+                spread = jnp.concatenate(
+                    [jnp.where(here, value[tt : tt + 1, :], 0.0) for tt in range(2)], axis=0
+                )
+                parts.append(jnp.concatenate(two_parts(spread), axis=0))
         placed = lax.dot_general(
-            jnp.concatenate(parts, axis=1), hot_low[chip], (((1,), (1,)), ((), ())),
-            preferred_element_type=F32,
+            jnp.concatenate(parts, axis=1),
+            jnp.concatenate([hot_low[chip] for chip in group], axis=1),
+            (((1,), (1,)), ((), ())), preferred_element_type=F32,
         )
         grid[...] += placed[0:64] + placed[64:128]
 
     results = []
     for tt in range(2):
-        first = turned(dot_exact(const[128:256, 0:32], grid[tt * 32 : tt * 32 + 32, :]), sign)
-        results.append(first * const[256:320, :] + rotated(first) * const[320:384, :])
-    last = dot_exact(const[384:448, :], jnp.concatenate(results, axis=0), ((1,), (1,)))
+        terms = three_terms(grid[tt * 32 : tt * 32 + 32, :], 0)
+        first = turned(jnp.dot(factors[128:256, 0:96], terms, preferred_element_type=F32), sign)
+        results.append(three_terms(first * const[0:64, :] + rotated(first) * const[64:128, :], 1))
+    last = lax.dot_general(
+        factors[256:320, :], jnp.concatenate(results, axis=0), (((1,), (1,)), ((), ())),
+        preferred_element_type=F32,
+    )
     low, upp = last[0:32], last[32:64]
     left = lax.broadcasted_iota(I32, (32, 128), 1) < 64
     left_ref[0] = jnp.where(left, low, 0.0)
@@ -374,7 +391,7 @@
     left, right = pl.pallas_call(
         kernel,
         out_shape=[jax.ShapeDtypeStruct((2, 32, 128), F32)] * 2,
-        in_specs=[any_space] * 7,
+        in_specs=[any_space] * 8,
         out_specs=[pl.BlockSpec(memory_space=pltpu.VMEM)] * 2,
         scratch_shapes=[
             pltpu.VMEM((K, T, q), BF16),
@@ -383,7 +400,8 @@
             pltpu.VMEM((q // 128, 128), I32),
             pltpu.VMEM((q // 128, 128), I32),
             pltpu.VMEM((16, 128), I32),
-            pltpu.VMEM((448, 128), F32),
+            pltpu.VMEM((128, 128), F32),
+            pltpu.VMEM((320, 384), BF16),
             pltpu.VMEM((16, 40, 256), BF16),
             pltpu.VMEM((2, 24, q), F32),
             pltpu.VMEM((K, T, 128), F32),
@@ -393,13 +411,13 @@
             pltpu.VMEM((H * 8, 128), F32),
             pltpu.VMEM((4, 2 * H, 128), F32),
             pltpu.VMEM((4, 2 * H, 128), F32),
-            pltpu.VMEM((40, 128), F32),
+            pltpu.VMEM((48, 128), F32),
             pltpu.VMEM((BLKS, 2, 128), F32),
             pltpu.VMEM((BLKS, 2, 128), F32),
             pltpu.VMEM((4, 16, 128), I32),
             pltpu.VMEM((16, 128, 256), BF16),
             pltpu.VMEM((64, 128), F32),
-            dma((7,)),
+            dma((8,)),
             dma((1,)), dma((16,)), dma((3,)), dma((4,)), dma((3,)), dma((4,)), dma((2,)), dma((BLKS,)),
         ],
         compiler_params=pltpu.CompilerParams(
@@ -415,7 +433,7 @@
                 slot_col.reshape(q // 128, 128),
                 slot_ell.reshape(q // 128, 128),
                 order_of_column.reshape(16, 128),
-                jnp.asarray(constants()),
+                *constants(),
             )
         )
     )

time: 36 us -> 35.9 us (level)
  no operation moved by 1% of the time
where the time goes in v3:
time: 35.9 us; the launch traced here: 35.8 us
  Pallas kernels  35.1 us (98%)
  other arithmetic  0.62 us (2%)
    pallas_call x1, Pallas kernels, on_device(): pl.pallas_call(kernel, out_shape=[jax.ShapeDtypeStruct((2, 32, 128), F32)...  35.1 us

profile of v3, /device:TPU:1, one launch (start us, length us, event | category | flops | bytes accessed | tf_op | source)
XLA Modules:
  0.0 35.8 jit_solution(8385510380598892029)
XLA Ops:
  0.0 35.1 %shard_map.82 = (f32[2,32,128]{2,1,0:T(8,128)S(1)}, f32[2,32,128]{2,1,0:T(8,128)S(1)}) custom-call(bf16[17,32,4224]{2,1,0:T(8,128)(2,1)} %bitcast.6, f32[2,4224]{1,0:T(2,128)} %sky_hbm.1, f32[17,2,2048]{2,1,0:T(2,128)} %bitcast.7, s32[33,128]{1,0:T(8,128)} %bitcast.8, s32[33,128]{1,0:T(8,128)} %bitcast.9, s32[16,128]{1,0:T(8,128)} %bitcast.10, ...), custom_call_target="tpu_custom_call" | custom-call | tf_op jit(solution)/shard_map/pallas_call | solution.py:391
  35.1 0.6 %add.14 = f32[2,32,128]{2,1,0:T(8,128)} add(f32[2,32,128]{2,1,0:T(8,128)S(1)} %get-tuple-element.7, f32[2,32,128]{2,1,0:T(8,128)S(1)} %get-tuple-element.8) | non-fusion elementwise | flops 8192 | bytes 98304 | tf_op jit(solution)/shard_map/add | solution.py:440

commit v4 on v3

--- a/solution.py
+++ b/solution.py
@@ -16,32 +16,31 @@
 
 def build_table(beam, table):
     rows = jnp.concatenate([beam[:, 0, :], beam[:, 1, :], jnp.zeros((6, 2048), F32)], axis=0)
-    high = rows.astype(BF16)
-    low = (rows - high.astype(F32)).astype(BF16)
     for h in range(16):
-        span = slice(h * 128, h * 128 + 128)
-        table[h, :, 0:128] = high[:, span]
-        table[h, :, 128:256] = low[:, span]
-
-
-def gather_block(base, table, ell, sky, coef, row, cols):
-    n = 128 * cols
-    degree = jnp.concatenate([ell[pl.ds(row + c, 1), :] for c in range(cols)], axis=1)
-    low = degree & 127
-    high = (degree >> 7) - base
-    hot = (lax.broadcasted_iota(I32, (128, n), 0) == low).astype(F32).astype(BF16)
-    hot = jnp.concatenate([hot, hot], axis=0)
-    lhs = table[pl.ds(base, 10)].reshape(10 * 40, 256)
-    picked = jnp.dot(lhs, hot, preferred_element_type=F32)
-    total = jnp.zeros((40, n), F32)
-    for h in range(10):
-        total = jnp.where(high == h, picked[h * 40 : h * 40 + 40], total)
-    br, bi = total[0:17], total[17:34]
-    start = pl.multiple_of(row * 128, 128)
-    s0 = sky[0:1, pl.ds(start, n)]
-    s1 = sky[1:2, pl.ds(start, n)]
-    coef[0, 0:17, pl.ds(start, n)] = s0 * br - s1 * bi
-    coef[1, 0:17, pl.ds(start, n)] = s0 * bi + s1 * br
+        table[h] = rows[:, h * 128 : h * 128 + 128]
+
+
+def gather_block(base, table, ell, sky, coef, first, last):
+    for c in range(first, last):
+        degree = ell[c : c + 1, :]
+        low = jnp.broadcast_to(degree & 127, (8, 128))
+        high = jnp.broadcast_to((degree >> 7) - base, (8, 128))
+        hits = [high == h for h in range(10)]
+        groups = []
+        for g in range(5):
+            total = jnp.zeros((8, 128), F32)
+            for h in range(10):
+                rows = table[base + h, 8 * g : 8 * g + 8, :]
+                got = jnp.take_along_axis(rows, low, axis=1, mode="promise_in_bounds")
+                total = jnp.where(hits[h], got, total)
+            groups.append(total)
+        total = jnp.concatenate(groups, axis=0)
+        br, bi = total[0:17], total[17:34]
+        span = slice(c * 128, c * 128 + 128)
+        s0 = sky[0:1, span]
+        s1 = sky[1:2, span]
+        coef[0, 0:17, span] = s0 * br - s1 * bi
+        coef[1, 0:17, span] = s0 * bi + s1 * br
 
 
 def add_block(wig, coef, col, acc, row, cols):
@@ -63,12 +62,6 @@
     right = jnp.concatenate(rhs, axis=1)
     part = lax.dot_general(left, right, (((1,), (1,)), ((), ())), preferred_element_type=F32)
     acc[...] = part.reshape(K, T, 128)
-
-
-def gather_all(sky, beam, col, ell, table, coef):
-    build_table(beam, table)
-    base = jnp.minimum(jnp.min(jnp.where(col[...] >= 0, ell[...], 2047)) >> 7, 6)
-    gather_block(base, table, ell, sky, coef, 0, ell.shape[0])
 
 
 def add_all(wig, col, coef, acc):
@@ -174,7 +167,7 @@
         for i, (src, dst) in enumerate(
             [
                 (beam_hbm, beam), (ell_hbm, ell), (col_hbm, col), (sky_hbm, sky),
-                (const_hbm, const), (ooc_hbm, ooc), (factors_hbm, factors), (wig_hbm, wig),
+                (wig_hbm, wig), (ooc_hbm, ooc), (const_hbm, const), (factors_hbm, factors),
             ]
         )
     ]
@@ -192,10 +185,15 @@
     @pl.when(turned_run)
     def _():
         pl.semaphore_signal(barrier, inc=1, device_id=(other, b), device_id_type=MESH)
-    for load in loads[:-1]:
+    for load in loads[:4]:
         load.wait()
-    gather_all(sky, beam, col, ell, table, coef)
-    loads[-1].wait()
+    build_table(beam, table)
+    base = jnp.minimum(jnp.min(jnp.where(col[...] >= 0, ell[...], 2047)) >> 7, 6)
+    tiles = ell.shape[0]
+    ahead = 10
+    gather_block(base, table, ell, sky, coef, 0, ahead)
+    loads[4].wait()
+    gather_block(base, table, ell, sky, coef, ahead, tiles)
     add_all(wig, col, coef, acc)
 
     pl.semaphore_wait(barrier, len(peers) + jnp.where(turned_run, 1, 0).astype(I32))
@@ -226,6 +224,8 @@
     for copy in e_copies:
         copy.start()
 
+    for load in loads[5:]:
+        load.wait()
     lane = lax.broadcasted_iota(I32, (16, 128), 1)
     order = ooc[...]
     swapped = rotated(order)
@@ -402,7 +402,7 @@
             pltpu.VMEM((16, 128), I32),
             pltpu.VMEM((128, 128), F32),
             pltpu.VMEM((320, 384), BF16),
-            pltpu.VMEM((16, 40, 256), BF16),
+            pltpu.VMEM((16, 40, 128), F32),
             pltpu.VMEM((2, 24, q), F32),
             pltpu.VMEM((K, T, 128), F32),
             pltpu.VMEM((16, K - H, 2, 128), F32),

time: 35.9 us -> 35.6 us (level)
  no operation moved by 1% of the time
where the time goes in v4:
time: 35.6 us; the launch traced here: 35.5 us
  Pallas kernels  34.8 us (98%)
  other arithmetic  0.62 us (2%)
    pallas_call x1, Pallas kernels, on_device(): pl.pallas_call(kernel, out_shape=[jax.ShapeDtypeStruct((2, 32, 128), F32)...  34.8 us

profile of v4, /device:TPU:1, one launch (start us, length us, event | category | flops | bytes accessed | tf_op | source)
XLA Modules:
  0.0 35.5 jit_solution(6261829597005706218)
XLA Ops:
  0.0 34.8 %shard_map.82 = (f32[2,32,128]{2,1,0:T(8,128)S(1)}, f32[2,32,128]{2,1,0:T(8,128)S(1)}) custom-call(bf16[17,32,4224]{2,1,0:T(8,128)(2,1)} %bitcast.6, f32[2,4224]{1,0:T(2,128)} %sky_hbm.1, f32[17,2,2048]{2,1,0:T(2,128)} %bitcast.7, s32[33,128]{1,0:T(8,128)} %bitcast.8, s32[33,128]{1,0:T(8,128)} %bitcast.9, s32[16,128]{1,0:T(8,128)} %bitcast.10, ...), custom_call_target="tpu_custom_call" | custom-call | tf_op jit(solution)/shard_map/pallas_call | solution.py:391
  34.8 0.6 %add.14 = f32[2,32,128]{2,1,0:T(8,128)} add(f32[2,32,128]{2,1,0:T(8,128)S(1)} %get-tuple-element.7, f32[2,32,128]{2,1,0:T(8,128)S(1)} %get-tuple-element.8) | non-fusion elementwise | flops 8192 | bytes 98304 | tf_op jit(solution)/shard_map/add | solution.py:440
